TPU v7x, 32 devices: a whole 2x2x4 slice. The times are simulated.
32 devices in a mesh: section: 8 (over y, x, core), tp: 4 (over z).
Axes of the slice: x: 2, y: 2, z: 4, core: 2. Of those that a mesh axis runs over, the one named last changes fastest.
Arguments:
- param: float32 [512, 3584], P('section', 'tp'), may hold values from -4 to 4
- moment_one: float32 [512, 3584], P('section', 'tp'), may hold values from -2 to 2
- moment_two: float32 [512, 3584], P('section', 'tp'), may hold values from 0.001 to 1
- proj_grad: float32 [512, 3584], P('section', 'tp'), may hold values from -6 to 6
- embed_grad: bfloat16 [4096, 3584], P('section', 'tp'), may hold values from -6 to 6
- token_ids: int32 [4096], P('section'), may hold values from 0 to 511, as said below
- next_ids: int32 [4096], P('section'), may hold values from 0 to 511, as said below
Outputs:
- new_param: float32 [512, 3584], P('section', 'tp')
- new_moment_one: float32 [512, 3584], P('section', 'tp')
- new_moment_two: float32 [512, 3584], P('section', 'tp')
- next_rows: bfloat16 [4096, 3584], P('section')
Inputs may be any that keep to these rules, and one draw needn't show every extreme that they name: `token_ids`: in each section index's block of 512 tokens at most 128 ids fall into any one owner's run of 64 table rows (id // 64); in every draw some owner receives exactly 128 from every block. `next_ids`: the same bound of 128 a block and an owner holds, and is reached, as for token_ids.
All inputs are finite; a program needn't handle non-finite values.
Results may differ from a plain program's by a relative error of at most 0.001.
Values may be sent and summed in bfloat16 or wider, within the bound.
A program may use at most 64 MiB of HBM per device.

v0:
```python
import functools

import jax
import jax.numpy as jnp
from jax import lax
from jax.experimental import pallas as pl
from jax.experimental.pallas import tpu as pltpu
from jax.sharding import PartitionSpec as P

STEP = 1000
MESH = pl.DeviceIdType.MESH


def adam(param, moment_one, moment_two, grad):
    new_moment_one = 0.9 * moment_one + 0.1 * grad
    new_moment_two = 0.999 * moment_two + 0.001 * grad * grad
    first_fix = 1.0 - 0.9**STEP
    second_fix = 1.0 - 0.999**STEP
    new_param = param - 0.01 * (new_moment_one / first_fix) / (
        jnp.sqrt(new_moment_two / second_fix) + 1e-08
    )
    return new_param, new_moment_one, new_moment_two


def chunks_of(width):
    first = -(-(width // 2) // 128) * 128
    return ((0, first), (first, width - first))


def sync_kernel(
    ranks, ids_in, next_in, rows_in, param_in, one_in, two_in, proj_in,
    new_param_out, new_one_out, new_two_out, out_ref,
    new_param_ref, new_one_ref, new_two_ref, found0, found1, state_s, found_s,
    ids_ref, next_ref, rows_ref, param_ref, one_ref, two_ref, proj_ref, load_s,
    pick, mine0, mine1, theirs0, theirs1, from_core0, from_core1, from_chip0, from_chip1,
    table0, table1,
    core_s, core_r, chip_s, chip_r, z_s, z_r, x_s, x_r, y_s, y_r,
    across_s, across_r, pair_s, pair_r, pz_s, pz_r, px_s, px_r, py_s, py_r,
    pacross_s, pacross_r, ppair_s, ppair_r,
):
    rows, width = param_ref.shape
    quarter = rows // 4
    main = rows
    chunks = chunks_of(width)
    mine, theirs = (mine0, mine1), (theirs0, theirs1)
    from_core, from_chip = (from_core0, from_core1), (from_chip0, from_chip1)
    tables, found = (table0, table1), (found0, found1)
    me = lax.axis_index("section")
    z = lax.axis_index("tp")
    core = lax.rem(me, 2)
    x_bit = lax.rem(lax.div(me, 2), 2)
    y_bit = lax.div(me, 4)
    by_core = me + 1 - 2 * core
    by_x = me + 2 - 4 * x_bit
    by_y = me + 4 - 8 * y_bit
    by_both = by_x + by_y - me
    chips = (by_both, by_x, by_y, me)
    has_low, has_high = z > 0, z < ranks - 1
    loads = [
        pltpu.make_async_copy(src, dst, load_s.at[k])
        for k, (src, dst) in enumerate((
            (ids_in, ids_ref), (rows_in, rows_ref), (next_in, next_ref), (proj_in, proj_ref),
            (param_in, param_ref), (one_in, one_ref), (two_in, two_ref),
        ))
    ]
    for one in loads:
        one.start()

    barrier = pltpu.get_barrier_semaphore()
    for other in (by_core, by_x, by_y, by_both):
        pl.semaphore_signal(barrier, inc=1, device_id=(other, z), device_id_type=MESH)

    @pl.when(has_low)
    def _():
        pl.semaphore_signal(barrier, inc=1, device_id=(me, z - 1), device_id_type=MESH)

    @pl.when(has_high)
    def _():
        pl.semaphore_signal(barrier, inc=1, device_id=(me, z + 1), device_id_type=MESH)

    def picks(owner_core):
        local = lax.broadcasted_iota(jnp.int32, (rows, ids_ref.shape[1]), 0)
        hits = []
        for chip in chips:
            first = (lax.div(chip, 2) * 2 + owner_core) * rows
            hit = local == ids_ref[...] - first
            hits.append(jnp.where(hit, 1.0, 0.0).astype(jnp.bfloat16))
        return jnp.concatenate(hits, axis=0)

    def partial_sums(hits, c):
        begin, size = chunks[c]
        return jnp.dot(
            hits, rows_ref[:, begin : begin + size], preferred_element_type=jnp.float32
        ).reshape(len(chips), rows, size)

    def copy(src, dst, send, recv, section, tp):
        return pltpu.make_async_remote_copy(
            src_ref=src, dst_ref=dst, send_sem=send, recv_sem=recv,
            device_id=(section, tp), device_id_type=MESH,
        )

    to_core = [
        [
            copy(theirs[c].at[k], from_core[c].at[k], core_s.at[c, k], core_r.at[c, k], by_core, z)
            for k in range(4)
        ]
        for c in range(2)
    ]
    to_chip = [
        [
            copy(mine[c].at[k], from_chip[c].at[k], chip_s.at[c, k], chip_r.at[c, k], chips[k], z)
            for k in range(3)
        ]
        for c in range(2)
    ]
    loads[0].wait()
    hits = picks(1 - core)
    loads[1].wait()
    theirs[0][...] = partial_sums(hits, 0)
    pl.semaphore_wait(
        barrier, 4 + has_low.astype(jnp.int32) + has_high.astype(jnp.int32)
    )
    for one in to_core[0]:
        one.start()
    theirs[1][...] = partial_sums(hits, 1)
    for one in to_core[1]:
        one.start()
    hits = picks(core)
    for c in range(2):
        mine[c][...] = partial_sums(hits, c)
        for k in range(3):
            to_core[c][k].wait_recv()
            mine[c][k] = mine[c][k] + from_core[c][k]
            to_chip[c][k].start()
    for one in loads[2:]:
        one.wait()
    index = lax.broadcasted_iota(jnp.int32, (pick.shape[1], pick.shape[0]), 0)
    pick[...] = jnp.where(index == next_ref[...], 1.0, 0.0).T.astype(jnp.bfloat16)

    def update(c):
        begin, size = chunks[c]
        cols = slice(begin, begin + size)
        to_core[c][3].wait_recv()
        total = proj_ref[:, cols] + (mine[c][3] + from_core[c][3])
        for k in (1, 2, 0):
            to_chip[c][k].wait_recv()
            total = total + from_chip[c][k]
        new_param, new_one, new_two = adam(
            param_ref[:, cols], one_ref[:, cols], two_ref[:, cols], total
        )
        tables[c][z, pl.ds(pl.multiple_of(me * rows, rows), rows)] = new_param.astype(jnp.bfloat16)
        new_param_ref[:, cols] = new_param
        new_one_ref[:, cols] = new_one
        new_two_ref[:, cols] = new_two

    def at(c, origin, section, first, size):
        begin = pl.multiple_of(section * rows + first, quarter)
        return tables[c].at[origin, pl.ds(begin, size)]

    def same(ref, send, recv, section, tp):
        return copy(ref, ref, send, recv, section, tp)

    states = [
        pltpu.make_async_copy(src, dst, state_s.at[k])
        for k, (src, dst) in enumerate((
            (new_param_ref, new_param_out), (new_one_ref, new_one_out), (new_two_ref, new_two_out),
        ))
    ]

    def main_z(c, o, up):
        return same(
            at(c, o, me, 0, main), z_s.at[c, up, o], z_r.at[c, o], me, z + 2 * up - 1
        )

    def main_x(c, o):
        return same(at(c, o, me, 0, main), x_s.at[c, o], x_r.at[c, o], by_x, z)

    def main_y(c, o):
        return same(at(c, o, me, 0, main), y_s.at[c, o], y_r.at[c, o], by_y, z)

    def main_across(c, o, from_x):
        first, size = (0, rows // 2) if from_x else (rows // 2, rows // 2)
        source, target = (by_x, by_y) if from_x else (by_y, by_x)
        k = int(from_x)
        return same(
            at(c, o, source, first, size), across_s.at[c, k, o], across_r.at[c, k, o], target, z
        )

    def main_pair(c, o, k, section=None):
        section = chips[k] if section is None else section
        return same(
            at(c, o, section, 0, main), pair_s.at[c, k, o], pair_r.at[c, k, o], by_core, z
        )

    def rest_x(c):
        return same(at(c, z, me, main, quarter), px_s.at[c], px_r.at[c], by_x, z)

    def rest_y(c):
        return same(at(c, z, me, main, quarter), py_s.at[c], py_r.at[c], by_y, z)

    def rest_across(c):
        source, target = (by_y, by_x) if c == 0 else (by_x, by_y)
        return same(at(c, z, source, main, quarter), pacross_s.at[c], pacross_r.at[c], target, z)

    def rest_z(c, o, k, up):
        return same(
            at(c, o, chips[k], main, quarter), pz_s.at[c, k, up, o], pz_r.at[c, k, o],
            me, z + 2 * up - 1,
        )

    def rest_pair(c, o, k, section=None):
        section = chips[k] if section is None else section
        return same(
            at(c, o, section, main, quarter), ppair_s.at[c, k, o], ppair_r.at[c, k, o], by_core, z
        )

    def both_z(make):
        pl.when(has_low)(lambda: make(0).start())
        pl.when(has_high)(lambda: make(1).start())

    def begin_gather(c):
        both_z(lambda up: main_z(c, z, up))
        main_x(c, z).start()
        main_y(c, z).start()
        main_pair(c, z, 3).start()

    def rest_near(c):
        for k in ((2, 1) if c == 0 else (1, 2)):
            (rest_x, rest_y)[k - 1](c).wait_recv()
            if k == (2 if c == 0 else 1):
                rest_across(c).start()
            both_z(lambda up: rest_z(c, z, k, up))
            rest_pair(c, z, k).start()

    def rest_far(c):
        rest_across(c).wait_recv()
        both_z(lambda up: rest_z(c, z, 0, up))
        rest_pair(c, z, 0).start()

    def sides(body, distance):
        if distance >= ranks:
            return
        if distance == 0:
            body(z, 0)
            return
        pl.when(z >= distance)(lambda: body(z - distance, 1))
        pl.when(z + distance < ranks)(lambda: body(z + distance, -1))

    def main_from_z(c, distance):
        def body(o, way):
            ref = at(c, o, me, 0, main)
            same(ref, z_s.at[c, 0, o], z_r.at[c, o], me, z - way).wait_recv()
            if way > 0:
                pl.when(has_high)(lambda: main_z(c, o, 1).start())
            else:
                pl.when(has_low)(lambda: main_z(c, o, 0).start())
            main_x(c, o).start()
            main_y(c, o).start()
            main_pair(c, o, 3).start()

        sides(body, distance)

    def rest_from_z(c, distance):
        def body(o, way):
            for k in (3, 1, 2, 0):
                ref = at(c, o, chips[k], main, quarter)
                same(ref, pz_s.at[c, k, 0, o], pz_r.at[c, k, o], me, z - way).wait_recv()
                if way > 0:
                    pl.when(has_high)(lambda: rest_z(c, o, k, 1).start())
                else:
                    pl.when(has_low)(lambda: rest_z(c, o, k, 0).start())
                rest_pair(c, o, k).start()

        sides(body, distance)

    def main_near(c, distance):
        def body(o, way):
            del way
            main_x(c, o).wait_recv()
            main_across(c, o, True).start()
            main_pair(c, o, 1).start()
            main_y(c, o).wait_recv()
            main_across(c, o, False).start()
            main_pair(c, o, 2).start()

        sides(body, distance)

    def main_far(c, distance):
        def body(o, way):
            del way
            main_across(c, o, True).wait_recv()
            main_across(c, o, False).wait_recv()
            main_pair(c, o, 0).start()

        sides(body, distance)

    origins, count = [0] * ranks, 0
    for distance in range(ranks):
        for way in ((0,) if distance == 0 else (-1, 1)):
            value = z + way * distance
            valid = ((value >= 0) & (value < ranks)).astype(jnp.int32)
            for k in range(ranks):
                same_rank = (count == k) if isinstance(count, int) else (count == k).astype(jnp.int32)
                origins[k] = origins[k] + valid * same_rank * value
            count = count + valid

    def found_copy(c, nearest):
        begin, size = chunks[c]
        start = pl.multiple_of(origins[nearest] * width + begin, 128)
        return pltpu.make_async_copy(
            found[c].at[nearest], out_ref.at[:, pl.ds(start, size)], found_s.at[c, nearest]
        )

    def choose(c, nearest):
        if nearest >= ranks:
            return
        o = origins[nearest]
        for k in range(4):
            other = chips[k] + 1 - 2 * core
            main_pair(c, o, k, other).wait_recv()
        found[c][nearest] = jnp.dot(
            pick[...], tables[c][o], preferred_element_type=jnp.float32
        ).astype(jnp.bfloat16)
        found_copy(c, nearest).start()

    update(0)
    begin_gather(0)
    main_from_z(0, 1)
    update(1)
    begin_gather(1)
    for one in states:
        one.start()
    main_from_z(0, 2)
    main_near(0, 0)
    main_from_z(1, 1)
    main_from_z(0, 3)
    main_near(0, 1)
    main_far(0, 0)
    main_from_z(1, 2)
    main_near(1, 0)
    main_near(0, 2)
    main_far(0, 1)
    main_from_z(1, 3)
    choose(0, 0)
    main_near(1, 1)
    main_far(1, 0)
    main_near(0, 3)
    main_far(0, 2)
    choose(0, 1)
    main_near(1, 2)
    main_far(1, 1)
    choose(1, 0)
    main_far(0, 3)
    choose(0, 2)
    main_near(1, 3)
    main_far(1, 2)
    choose(1, 1)
    choose(0, 3)
    choose(1, 2)
    for late in range(4, ranks):
        for c in range(2):
            main_from_z(c, late)
            main_near(c, late)
            main_far(c, late)
            choose(c, late)
    main_far(1, 3)
    choose(1, 3)

    for one in states:
        one.wait()
    for c in range(2):
        for nearest in range(ranks):
            found_copy(c, nearest).wait()
        for one in to_core[c] + to_chip[c]:
            one.wait_send()
        for o in range(ranks):
            for k in range(4):
                main_pair(c, o, k).wait_send()
            main_x(c, o).wait_send()
            main_y(c, o).wait_send()
            main_across(c, o, True).wait_send()
            main_across(c, o, False).wait_send()

            def down(c=c, o=o):
                main_z(c, o, 0).wait_send()

            def up(c=c, o=o):
                main_z(c, o, 1).wait_send()

            pl.when((o >= z) & has_low)(down)
            pl.when((o <= z) & has_high)(up)


def fused(ranks, param, moment_one, moment_two, proj_grad, embed_grad, token_ids, next_ids):
    rows, width = param.shape
    owners = lax.axis_size("section")
    tokens = token_ids.shape[0]
    table_rows = owners * rows
    dma = pltpu.SemaphoreType.DMA
    own = jax.ShapeDtypeStruct((rows, width), jnp.float32)
    sizes = [size for _, size in chunks_of(width)]

    def sums(count):
        return [pltpu.VMEM((count, rows, size), jnp.float32) for size in sizes]

    results = pl.pallas_call(
        functools.partial(sync_kernel, ranks),
        out_shape=(own, own, own, jax.ShapeDtypeStruct((tokens, ranks * width), jnp.bfloat16)),
        in_specs=[pl.BlockSpec(memory_space=pltpu.HBM)] * 7,
        out_specs=(pl.BlockSpec(memory_space=pltpu.HBM),) * 4,
        scratch_shapes=[
            *[pltpu.VMEM((rows, width), jnp.float32)] * 3,
            *[pltpu.VMEM((ranks, tokens, size), jnp.bfloat16) for size in sizes],
            dma((3,)), dma((2, ranks)),
            pltpu.VMEM((1, tokens), jnp.int32), pltpu.VMEM((1, tokens), jnp.int32),
            pltpu.VMEM((tokens, width), jnp.bfloat16),
            *[pltpu.VMEM((rows, width), jnp.float32)] * 4, dma((7,)),
            pltpu.VMEM((tokens, table_rows), jnp.bfloat16),
            *sums(4), *sums(4), *sums(4), *sums(3),
            *[pltpu.VMEM((ranks, table_rows, size), jnp.bfloat16) for size in sizes],
            dma((2, 4)), dma((2, 4)), dma((2, 3)), dma((2, 3)),
            dma((2, 2, ranks)), dma((2, ranks)),
            dma((2, ranks)), dma((2, ranks)), dma((2, ranks)), dma((2, ranks)),
            dma((2, 2, ranks)), dma((2, 2, ranks)), dma((2, 4, ranks)), dma((2, 4, ranks)),
            dma((2, 4, 2, ranks)), dma((2, 4, ranks)),
            dma((2,)), dma((2,)), dma((2,)), dma((2,)), dma((2,)), dma((2,)),
            dma((2, 4, ranks)), dma((2, 4, ranks)),
        ],
        compiler_params=pltpu.CompilerParams(collective_id=0, has_side_effects=True),
    )(
        token_ids.reshape(1, tokens), next_ids.reshape(1, tokens), embed_grad,
        param, moment_one, moment_two, proj_grad,
    )
    steps = 8
    blocks = [
        pl.BlockSpec((one.shape[0] // steps, one.shape[1]), lambda i: (i, 0)) for one in results
    ]
    return pl.pallas_call(
        hand_over,
        grid=(steps,),
        out_shape=tuple(jax.ShapeDtypeStruct(one.shape, one.dtype) for one in results),
        in_specs=blocks,
        out_specs=blocks,
    )(*results)


def hand_over(*refs):
    for src, dst in zip(refs[:4], refs[4:]):
        dst[...] = src[...]


def slot_layout(ids, owners, cap, rows_own):
    owner = ids // rows_own
    hits = (owner[:, None] == jnp.arange(owners)[None, :]).astype(jnp.int32)
    before = jnp.cumsum(hits, axis=0) - hits
    rank = jnp.sum(before * hits, axis=1)
    return (owner * cap + rank, ids - owner * rows_own)


def exchange(param, moment_one, moment_two, proj_grad, embed_grad, token_ids, next_ids):
    rows_own, width = param.shape
    owners = lax.axis_size("section")
    tokens_here = token_ids.shape[0]
    cap = 2 * tokens_here // owners
    slot, local = slot_layout(token_ids, owners, cap, rows_own)
    outgoing = jnp.zeros((owners * cap, width), jnp.bfloat16).at[slot].set(embed_grad)
    targets = jnp.full((owners * cap,), -1, jnp.int32).at[slot].set(local)
    got_rows, got_local = (
        lax.all_to_all(
            outgoing.reshape(owners, cap, width), "section", split_axis=0, concat_axis=0, tiled=True
        ),
        lax.all_to_all(
            targets.reshape(owners, cap), "section", split_axis=0, concat_axis=0, tiled=True
        ),
    )
    select = (jnp.arange(rows_own)[:, None] == got_local.reshape(-1)[None, :]).astype(jnp.bfloat16)
    embed_sum = jnp.dot(
        select, got_rows.reshape(owners * cap, width), preferred_element_type=jnp.float32
    )
    grad = proj_grad + embed_sum
    new_param, new_moment_one, new_moment_two = adam(param, moment_one, moment_two, grad)
    table = new_param.astype(jnp.bfloat16)
    piece = lax.all_gather(table, "section", axis=0, tiled=True)
    inside = (next_ids >= 0) & (next_ids < piece.shape[0])
    found = jnp.take(piece, jnp.clip(next_ids, 0, piece.shape[0] - 1), axis=0)
    mine = jnp.where(inside[:, None], found, jnp.zeros((tokens_here, width), jnp.bfloat16))
    next_rows = lax.all_gather(mine, "tp", axis=1, tiled=True)
    return (new_param, new_moment_one, new_moment_two, next_rows)


def solution(mesh):
    placed = (
        P("section", "tp"),
        P("section", "tp"),
        P("section", "tp"),
        P("section", "tp"),
        P("section", "tp"),
        P("section"),
        P("section"),
    )
    ranks = mesh.shape["tp"]

    def on_device(*args):
        owners = mesh.shape["section"]
        table_rows, tokens = args[0].shape[0] * owners, args[5].shape[0]
        if owners == 2 ** 3 and table_rows <= tokens and args[0].shape[0] % 64 == 0 and args[0].shape[1] % 256 in (0, 128):
            return fused(ranks, *args)
        return exchange(*args)

    return jax.shard_map(
        on_device,
        mesh=mesh,
        in_specs=placed,
        out_specs=(P("section", "tp"), P("section", "tp"), P("section", "tp"), P("section", None)),
        check_vma=False,
    )
```

profile of v0, /device:TPU:1, one launch (start us, length us, event | category | flops | bytes accessed | tf_op | source)
XLA Modules:
  0.0 49.4 jit_solution(5884862312681920124)
XLA Ops:
  0.6 42.1 %shard_map.102 = (f32[64,896]{1,0:T(8,128)}, f32[64,896]{1,0:T(8,128)}, f32[64,896]{1,0:T(8,128)}, bf16[512,3584]{1,0:T(8,128)(2,1)}) custom-call(s32[1,512]{1,0:T(1,128)} %bitcast.2, s32[1,512]{1,0:T(1,128)} %bitcast.3, bf16[512,896]{1,0:T(8,128)(2,1)} %rows_in.1, f32[64,896]{1,0:T(8,128)} %param_in.1, f32[64,896]{1,0:T(8,128)} %one_in.1, ...), custom_call_target="tpu_custom_call" | custom-call | tf_op jit(solution)/shard_map/pallas_call | solution.py:406
  42.8 6.7 %shard_map.103 = (f32[64,896]{1,0:T(8,128)}, f32[64,896]{1,0:T(8,128)}, f32[64,896]{1,0:T(8,128)}, bf16[512,3584]{1,0:T(8,128)(2,1)}) custom-call(f32[64,896]{1,0:T(8,128)} %get-tuple-element.8.refs_0_, f32[64,896]{1,0:T(8,128)} %get-tuple-element.9.refs_1_, f32[64,896]{1,0:T(8,128)} %get-tuple-element.10.refs_2_, bf16[512,3584]{1,0:T(8,128)(2,1)} %get-tuple-element.11.refs_3_), custom_call_target="tpu_custom_call" | custom-call | tf_op jit(solution)/shard_map/pallas_call | solution.py:438
where the time goes:
time: 49.7 us; the launch traced here: 49.4 us
  Pallas kernels  48.8 us (98%)
  between operations  0.64 us (1%)
    pallas_call x1, Pallas kernels, fused(): pl.pallas_call(functools.partial(sync_kernel, ranks), out_shape=(own, own...  42.1 us
    pallas_call x1, Pallas kernels, fused(): pl.pallas_call(hand_over, grid=(steps,), out_shape=tuple((jax.ShapeDtypeS...  6.67 us

commit v1 on v0

--- a/solution.py
+++ b/solution.py
@@ -397,7 +397,7 @@
     tokens = token_ids.shape[0]
     table_rows = owners * rows
     dma = pltpu.SemaphoreType.DMA
-    own = jax.ShapeDtypeStruct((rows, width), jnp.float32)
+    own = pltpu.VMEM((rows, width), jnp.float32)
     sizes = [size for _, size in chunks_of(width)]
 
     def sums(count):
@@ -405,9 +405,9 @@
 
     results = pl.pallas_call(
         functools.partial(sync_kernel, ranks),
-        out_shape=(own, own, own, jax.ShapeDtypeStruct((tokens, ranks * width), jnp.bfloat16)),
+        out_shape=(own, own, own, pltpu.VMEM((tokens, ranks * width), jnp.bfloat16)),
         in_specs=[pl.BlockSpec(memory_space=pltpu.HBM)] * 7,
-        out_specs=(pl.BlockSpec(memory_space=pltpu.HBM),) * 4,
+        out_specs=(pl.BlockSpec(memory_space=pltpu.VMEM),) * 4,
         scratch_shapes=[
             *[pltpu.VMEM((rows, width), jnp.float32)] * 3,
             *[pltpu.VMEM((ranks, tokens, size), jnp.bfloat16) for size in sizes],
@@ -426,27 +426,34 @@
             dma((2,)), dma((2,)), dma((2,)), dma((2,)), dma((2,)), dma((2,)),
             dma((2, 4, ranks)), dma((2, 4, ranks)),
         ],
-        compiler_params=pltpu.CompilerParams(collective_id=0, has_side_effects=True),
-    )(
-        token_ids.reshape(1, tokens), next_ids.reshape(1, tokens), embed_grad,
-        param, moment_one, moment_two, proj_grad,
-    )
-    steps = 8
-    blocks = [
-        pl.BlockSpec((one.shape[0] // steps, one.shape[1]), lambda i: (i, 0)) for one in results
-    ]
+        compiler_params=pltpu.CompilerParams(collective_id=0, has_side_effects=True, vmem_limit_bytes=48 * 2 ** 20),
+    )(*(
+        pltpu.with_memory_space_constraint(one, pltpu.HBM)
+        for one in (
+            token_ids.reshape(1, tokens), next_ids.reshape(1, tokens), embed_grad,
+            param, moment_one, moment_two, proj_grad,
+        )
+    ))
     return pl.pallas_call(
         hand_over,
-        grid=(steps,),
         out_shape=tuple(jax.ShapeDtypeStruct(one.shape, one.dtype) for one in results),
-        in_specs=blocks,
-        out_specs=blocks,
-    )(*results)
+        in_specs=[pl.BlockSpec(memory_space=pltpu.VMEM)] * 4,
+        out_specs=(pl.BlockSpec(memory_space=pltpu.HBM),) * 4,
+        scratch_shapes=[dma((4,))],
+        compiler_params=pltpu.CompilerParams(vmem_limit_bytes=16 * 2 ** 20),
+    )(*(pltpu.with_memory_space_constraint(one, pltpu.VMEM) for one in results))
 
 
 def hand_over(*refs):
-    for src, dst in zip(refs[:4], refs[4:]):
-        dst[...] = src[...]
+    done = refs[8]
+    copies = [
+        pltpu.make_async_copy(src, dst, done.at[k])
+        for k, (src, dst) in enumerate(zip(refs[:4], refs[4:8]))
+    ]
+    for one in copies[::-1]:
+        one.start()
+    for one in copies:
+        one.wait()
 
 
 def slot_layout(ids, owners, cap, rows_own):

time: 49.7 us -> 44.4 us (0.89)
  the two profiles are of different devices: /device:TPU:1 before, /device:TPU:0 now
where the time goes in v1:
time: 44.4 us; the launch traced here: 43.8 us
  Pallas kernels  43.1 us (97%)
  between operations  0.64 us (1%)
    pallas_call x1, Pallas kernels, fused(): pl.pallas_call(functools.partial(sync_kernel, ranks), out_shape=(own, own...  41.1 us
    pallas_call x1, Pallas kernels, fused(): pl.pallas_call(hand_over, out_shape=tuple((jax.ShapeDtypeStruct(one.shape...  2.09 us

profile of v1, /device:TPU:0, one launch (start us, length us, event | category | flops | bytes accessed | tf_op | source)
XLA Modules:
  0.0 43.8 jit_solution(7145016095685783117)
XLA Ops:
  0.6 41.1 %shard_map.102 = (f32[64,896]{1,0:T(8,128)S(1)}, f32[64,896]{1,0:T(8,128)S(1)}, f32[64,896]{1,0:T(8,128)S(1)}, bf16[512,3584]{1,0:T(8,128)(2,1)S(1)}) custom-call(s32[1,512]{1,0:T(1,128)} %bitcast.2, s32[1,512]{1,0:T(1,128)} %bitcast.3, bf16[512,896]{1,0:T(8,128)(2,1)} %rows_in.1, f32[64,896]{1,0:T(8,128)} %param_in.1, f32[64,896]{1,0:T(8,128)} %one_in.1, ...), custom_call_target="tpu_custom_call" | custom-call | tf_op jit(solution)/shard_map/pallas_call | solution.py:406
  41.7 2.1 %shard_map.103 = (f32[64,896]{1,0:T(8,128)}, f32[64,896]{1,0:T(8,128)}, f32[64,896]{1,0:T(8,128)}, bf16[512,3584]{1,0:T(8,128)(2,1)}) custom-call(f32[64,896]{1,0:T(8,128)S(1)} %get-tuple-element.8.refs_0_, f32[64,896]{1,0:T(8,128)S(1)} %get-tuple-element.9.refs_1_, f32[64,896]{1,0:T(8,128)S(1)} %get-tuple-element.10.refs_2_, ...), custom_call_target="tpu_custom_call" | custom-call | tf_op jit(solution)/shard_map/pallas_call | solution.py:437

commit v2 on v1

v2 whole, which is shorter than its diff:
```python
import functools

import jax
import jax.numpy as jnp
from jax import lax
from jax.experimental import pallas as pl
from jax.experimental.pallas import tpu as pltpu
from jax.sharding import PartitionSpec as P

STEP = 1000
MESH = pl.DeviceIdType.MESH


def adam(param, moment_one, moment_two, grad):
    new_moment_one = 0.9 * moment_one + 0.1 * grad
    new_moment_two = 0.999 * moment_two + 0.001 * grad * grad
    first_fix = 1.0 - 0.9**STEP
    second_fix = 1.0 - 0.999**STEP
    new_param = param - 0.01 * (new_moment_one / first_fix) / (
        jnp.sqrt(new_moment_two / second_fix) + 1e-08
    )
    return new_param, new_moment_one, new_moment_two


STEPS = 32000.0


def chunks_of(width):
    first = -(-(width // 2) // 128) * 128
    return ((0, first), (first, width - first))


def sync_kernel(
    ranks, ids_in, next_in, rows_in, param_in, one_in, two_in, proj_in,
    new_param_ref, new_one_ref, new_two_ref, out_ref,
    ids_ref, next_ref, rows0, rows1, state_ref, pick, part0, part1, code0, code1, scale0, scale1,
    got0, got1, got_scale0, got_scale1, table0, table1,
    load_s, core_s, core_r, chip_s, chip_r, z_r, near_r, far_r, rest_r, rest_z_r, pair_r,
    main_s, rest_s, pair_s, z_s,
):
    rows, width = new_param_ref.shape
    rest = rows // 4
    main = rows - rest
    chunks = chunks_of(width)
    tokens_of, part, tables = (rows0, rows1), (part0, part1), (table0, table1)
    code, scale = (code0, code1), (scale0, scale1)
    got, got_scale = (got0, got1), (got_scale0, got_scale1)
    me = lax.axis_index("section")
    z = lax.axis_index("tp")
    core = lax.rem(me, 2)
    x_bit = lax.rem(lax.div(me, 2), 2)
    y_bit = lax.div(me, 4)
    by_core = me + 1 - 2 * core
    by_x = me + 2 - 4 * x_bit
    by_y = me + 4 - 8 * y_bit
    by_both = by_x + by_y - me
    sections = (by_both, by_x, by_y, me)
    chips = tuple(lax.div(one, 2) for one in sections)
    has_low, has_high = z > 0, z < ranks - 1

    def load(src, dst, k):
        return pltpu.make_async_copy(src, dst, load_s.at[k])

    loads = [load(ids_in, ids_ref.at[0], 0)] + [
        load(rows_in.at[:, pl.ds(begin, size)], tokens_of[c].at[0], 1 + c)
        for c, (begin, size) in enumerate(chunks)
    ]
    late = [load(next_in, next_ref, 3)] + [
        load(src, state_ref.at[k], 4) for k, src in enumerate((param_in, one_in, two_in, proj_in))
    ]
    for one in loads + late:
        one.start()

    barrier = pltpu.get_barrier_semaphore()
    for other in (by_core, by_x, by_y, by_both):
        pl.semaphore_signal(barrier, inc=1, device_id=(other, z), device_id_type=MESH)

    @pl.when(has_low)
    def _():
        pl.semaphore_signal(barrier, inc=1, device_id=(me, z - 1), device_id_type=MESH)

    @pl.when(has_high)
    def _():
        pl.semaphore_signal(barrier, inc=1, device_id=(me, z + 1), device_id_type=MESH)

    def copy(src, dst, send, recv, section, tp):
        return pltpu.make_async_remote_copy(
            src_ref=src, dst_ref=dst, send_sem=send, recv_sem=recv,
            device_id=(section, tp), device_id_type=MESH,
        )

    def arrived(ref, semaphore):
        pltpu.make_async_copy(ref, ref, semaphore).wait()

    def hits_of(slot):
        ids = ids_ref[slot]
        local = lax.broadcasted_iota(jnp.int32, (rows, ids.shape[1]), 0)
        return jnp.concatenate(
            [
                jnp.where(local == ids - (2 * chip + core) * rows, 1.0, 0.0).astype(jnp.bfloat16)
                for chip in chips
            ],
            axis=0,
        )

    to_core = [copy(ids_ref.at[0], ids_ref.at[1], core_s.at[2], core_r.at[2], by_core, z)] + [
        copy(one.at[0], one.at[1], core_s.at[c], core_r.at[c], by_core, z)
        for c, one in enumerate(tokens_of)
    ]
    loads[0].wait()
    own_hits = hits_of(0)
    pl.semaphore_wait(
        barrier, 4 + has_low.astype(jnp.int32) + has_high.astype(jnp.int32)
    )
    to_core[0].start()
    for c in range(2):
        loads[1 + c].wait()
        to_core[1 + c].start()

    def own_sums(c):
        part[c][...] = jnp.dot(
            own_hits, tokens_of[c][0], preferred_element_type=jnp.float32
        ).reshape(part[c].shape)

    def send_sums(c):
        to_core[1 + c].wait_recv()
        part[c][...] += jnp.dot(
            other_hits, tokens_of[c][1], preferred_element_type=jnp.float32
        ).reshape(part[c].shape)
        for k in range(3):
            sums = part[c][k]
            top = jnp.maximum(jnp.max(jnp.abs(sums), axis=0, keepdims=True), 1e-30)
            code[c][k] = jnp.round(sums * (STEPS / top)).astype(jnp.int32).astype(jnp.int16)
            scale[c][k] = top * (1.0 / STEPS)
            copy(
                code[c].at[k], got[c].at[k], chip_s.at[c, 0], chip_r.at[c, 0], sections[k], z
            ).start()
            copy(
                scale[c].at[k], got_scale[c].at[k], chip_s.at[c, 1], chip_r.at[c, 1], sections[k], z
            ).start()

    own_sums(0)
    to_core[0].wait_recv()
    other_hits = hits_of(1)
    send_sums(0)
    own_sums(1)
    send_sums(1)
    late[0].wait()
    index = lax.broadcasted_iota(jnp.int32, (pick.shape[1], pick.shape[0]), 0)
    pick[...] = jnp.where(index == next_ref[...], 1.0, 0.0).T.astype(jnp.bfloat16)
    arrived(state_ref, load_s.at[4])

    def at(c, o, chip, first, size):
        return tables[c].at[o, chip, core, pl.ds(first, size)]

    def mains(c, count, chip_count=1):
        return tables[c].at[pl.ds(0, count), pl.ds(0, chip_count), 0, pl.ds(0, main)]

    def rests(c, count, chip_count=4):
        return tables[c].at[pl.ds(0, count), pl.ds(0, chip_count), 0, pl.ds(main, rest)]

    def same(ref, send, recv, section, tp):
        copy(ref, ref, send, recv, section, tp).start()

    def to_pair(c, o, chip, first, size):
        same(at(c, o, chip, first, size), pair_s.at[c], pair_r.at[c, o], by_core, z)

    def to_x(c, o, chip, first, size, send, recv):
        same(at(c, o, chip, first, size), send, recv, by_x, z)

    def to_y(c, o, chip, first, size, send, recv):
        same(at(c, o, chip, first, size), send, recv, by_y, z)

    def along_z(c, kind, ref, recv, way):
        def up():
            same(ref, z_s.at[c, kind, 1], recv, me, z + 1)

        def down():
            same(ref, z_s.at[c, kind, 0], recv, me, z - 1)

        if way >= 0:
            pl.when(has_high)(up)
        if way <= 0:
            pl.when(has_low)(down)

    def spread_main(c, o, way):
        ref = at(c, o, chips[3], 0, main)
        along_z(c, 0, ref, z_r.at[c, o], way)
        to_x(c, o, chips[3], 0, main, main_s.at[c], near_r.at[c, o])
        to_y(c, o, chips[3], 0, main, main_s.at[c], near_r.at[c, o])

    def update(c):
        begin, size = chunks[c]
        cols = slice(begin, begin + size)
        total = state_ref[3, :, cols] + part[c][3]
        arrived(got[c], chip_r.at[c, 0])
        arrived(got_scale[c], chip_r.at[c, 1])
        for k in range(3):
            total = total + got[c][k].astype(jnp.int32).astype(jnp.float32) * got_scale[c][k]
        new_param, new_one, new_two = adam(
            state_ref[0, :, cols], state_ref[1, :, cols], state_ref[2, :, cols], total
        )
        tables[c][z, chips[3], core] = new_param.astype(jnp.bfloat16)
        to_x(c, z, chips[3], main, rest, rest_s.at[c], rest_r.at[c, 0])
        to_y(c, z, chips[3], main, rest, rest_s.at[c], rest_r.at[c, 0])
        spread_main(c, z, 0)
        to_pair(c, z, chips[3], 0, rows)
        new_param_ref[:, cols] = new_param
        new_one_ref[:, cols] = new_one
        new_two_ref[:, cols] = new_two

    def sides(body, distance):
        if distance >= ranks:
            return
        if distance == 0:
            body(z, 0)
            return
        pl.when(z >= distance)(lambda: body(z - distance, 1))
        pl.when(z + distance < ranks)(lambda: body(z + distance, -1))

    def main_from_z(c, distance):
        def body(o, way):
            arrived(at(c, o, chips[3], 0, main), z_r.at[c, o])
            spread_main(c, o, way)
            to_pair(c, o, chips[3], 0, main)

        sides(body, distance)

    def main_near(c, distance):
        def body(o, way):
            del way
            arrived(mains(c, 1, 2), near_r.at[c, o])
            half = main // 32 * 16
            cuts = ((0, half), (half, main - half))
            to_y(c, o, chips[1], *cuts[c], main_s.at[c], far_r.at[c, o])
            to_x(c, o, chips[2], *cuts[1 - c], main_s.at[c], far_r.at[c, o])
            to_pair(c, o, chips[1], 0, main)
            to_pair(c, o, chips[2], 0, main)

        sides(body, distance)

    def main_far(c, distance):
        def body(o, way):
            del way
            arrived(mains(c, 1), far_r.at[c, o])
            to_pair(c, o, chips[0], 0, main)

        sides(body, distance)

    def rest_near(c):
        arrived(rests(c, 1, 2), rest_r.at[c, 0])
        if c == 0:
            to_y(c, z, chips[1], main, rest, rest_s.at[c], rest_r.at[c, 1])
        else:
            to_x(c, z, chips[2], main, rest, rest_s.at[c], rest_r.at[c, 1])
        to_pair(c, z, chips[1], main, rest)
        to_pair(c, z, chips[2], main, rest)

    def all_rest(c, o):
        return tables[c].at[o, pl.ds(0, 4), core, pl.ds(main, rest)]

    def rest_far(c):
        arrived(rests(c, 1, 1), rest_r.at[c, 1])
        along_z(c, 1, all_rest(c, z), rest_z_r.at[c, z], 0)
        to_pair(c, z, chips[0], main, rest)

    def rest_from_z(c, distance):
        def body(o, way):
            ref = all_rest(c, o)
            arrived(ref, rest_z_r.at[c, o])
            along_z(c, 1, ref, rest_z_r.at[c, o], way)
            same(ref, pair_s.at[c], pair_r.at[c, o], by_core, z)

        sides(body, distance)

    origins, count = [0] * ranks, 0
    for distance in range(ranks):
        for way in ((0,) if distance == 0 else (-1, 1)):
            value = z + way * distance
            valid = ((value >= 0) & (value < ranks)).astype(jnp.int32)
            for k in range(ranks):
                same_rank = (count == k) if isinstance(count, int) else (count == k).astype(jnp.int32)
                origins[k] = origins[k] + valid * same_rank * value
            count = count + valid

    def choose(c, nearest):
        if nearest >= ranks:
            return
        o = origins[nearest]
        arrived(tables[c].at[o, pl.ds(0, 4), 0], pair_r.at[c, o])
        begin, size = chunks[c]
        start = pl.multiple_of(o * width + begin, 128)
        out_ref[:, pl.ds(start, size)] = jnp.dot(
            pick[...], tables[c][o].reshape(pick.shape[1], size),
            preferred_element_type=jnp.float32,
        ).astype(jnp.bfloat16)

    update(0)
    rest_near(0)
    update(1)
    main_from_z(0, 1)
    rest_far(0)
    rest_near(1)
    main_from_z(1, 1)
    main_near(1, 0)
    main_from_z(0, 2)
    rest_far(1)
    main_near(0, 0)
    main_from_z(1, 2)
    main_near(0, 1)
    rest_from_z(0, 1)
    main_from_z(0, 3)
    rest_from_z(1, 1)
    main_from_z(1, 3)
    main_far(1, 0)
    main_near(0, 2)
    main_near(1, 1)
    rest_from_z(0, 2)
    main_far(0, 0)
    choose(1, 0)
    main_near(1, 2)
    main_near(0, 3)
    rest_from_z(1, 2)
    main_far(0, 1)
    main_near(1, 3)
    choose(0, 0)
    main_far(0, 2)
    main_far(1, 1)
    main_far(1, 2)
    choose(0, 1)
    main_far(0, 3)
    choose(1, 1)
    rest_from_z(0, 3)
    choose(1, 2)
    main_far(1, 3)
    rest_from_z(1, 3)
    choose(0, 2)
    choose(0, 3)
    choose(1, 3)

    for distance in range(4, ranks):
        for c in range(2):
            main_from_z(c, distance)
            main_near(c, distance)
            main_far(c, distance)
            rest_from_z(c, distance)
            choose(c, distance)

    for one in to_core:
        one.wait_send()
    for c in range(2):
        arrived(code[c], chip_s.at[c, 0])
        arrived(scale[c], chip_s.at[c, 1])
        arrived(mains(c, ranks, 3), main_s.at[c])
        arrived(rests(c, 1, 3), rest_s.at[c])
        arrived(tables[c].at[pl.ds(0, ranks), pl.ds(0, 4), 0], pair_s.at[c])
        for rank in range(ranks):
            def sent(c=c, rank=rank):
                for way, messages in ((1, rank + 1), (0, ranks - rank)):
                    if rank != (ranks - 1) * way:
                        arrived(mains(c, messages), z_s.at[c, 0, way])
                        arrived(rests(c, messages), z_s.at[c, 1, way])

            pl.when(z == rank)(sent)


def fused(ranks, param, moment_one, moment_two, proj_grad, embed_grad, token_ids, next_ids):
    rows, width = param.shape
    owners = lax.axis_size("section")
    tokens = token_ids.shape[0]
    table_rows = owners * rows
    dma = pltpu.SemaphoreType.DMA
    own = pltpu.VMEM((rows, width), jnp.float32)
    sizes = [size for _, size in chunks_of(width)]

    def both(*lead, dtype):
        return [pltpu.VMEM((*lead, size), dtype) for size in sizes]

    results = pl.pallas_call(
        functools.partial(sync_kernel, ranks),
        out_shape=(own, own, own, pltpu.VMEM((tokens, ranks * width), jnp.bfloat16)),
        in_specs=[pl.BlockSpec(memory_space=pltpu.HBM)] * 7,
        out_specs=(pl.BlockSpec(memory_space=pltpu.VMEM),) * 4,
        scratch_shapes=[
            pltpu.VMEM((2, 1, tokens), jnp.int32), pltpu.VMEM((1, tokens), jnp.int32),
            *both(2, tokens, dtype=jnp.bfloat16),
            pltpu.VMEM((4, rows, width), jnp.float32),
            pltpu.VMEM((tokens, table_rows), jnp.bfloat16),
            *both(4, rows, dtype=jnp.float32),
            *both(3, rows, dtype=jnp.int16), *both(3, 1, dtype=jnp.float32),
            *both(3, rows, dtype=jnp.int16), *both(3, 1, dtype=jnp.float32),
            *both(ranks, 4, 2, rows, dtype=jnp.bfloat16),
            dma((5,)), dma((3,)), dma((3,)), dma((2, 2)), dma((2, 2)),
            dma((2, ranks)), dma((2, ranks)), dma((2, ranks)), dma((2, 2)), dma((2, ranks)),
            dma((2, ranks)), dma((2,)), dma((2,)), dma((2,)), dma((2, 2, 2)),
        ],
        compiler_params=pltpu.CompilerParams(
            collective_id=0, has_side_effects=True, vmem_limit_bytes=48 * 2 ** 20
        ),
    )(*(
        pltpu.with_memory_space_constraint(one, pltpu.HBM)
        for one in (
            token_ids.reshape(1, tokens), next_ids.reshape(1, tokens), embed_grad,
            param, moment_one, moment_two, proj_grad,
        )
    ))
    return pl.pallas_call(
        hand_over,
        out_shape=tuple(jax.ShapeDtypeStruct(one.shape, one.dtype) for one in results),
        in_specs=[pl.BlockSpec(memory_space=pltpu.VMEM)] * 4,
        out_specs=(pl.BlockSpec(memory_space=pltpu.HBM),) * 4,
        scratch_shapes=[dma((4,))],
        compiler_params=pltpu.CompilerParams(vmem_limit_bytes=16 * 2 ** 20),
    )(*(pltpu.with_memory_space_constraint(one, pltpu.VMEM) for one in results))


def hand_over(*refs):
    done = refs[8]
    copies = [
        pltpu.make_async_copy(src, dst, done.at[k])
        for k, (src, dst) in enumerate(zip(refs[:4], refs[4:8]))
    ]
    for one in copies[::-1]:
        one.start()
    for one in copies:
        one.wait()


def slot_layout(ids, owners, cap, rows_own):
    owner = ids // rows_own
    hits = (owner[:, None] == jnp.arange(owners)[None, :]).astype(jnp.int32)
    before = jnp.cumsum(hits, axis=0) - hits
    rank = jnp.sum(before * hits, axis=1)
    return (owner * cap + rank, ids - owner * rows_own)


def exchange(param, moment_one, moment_two, proj_grad, embed_grad, token_ids, next_ids):
    rows_own, width = param.shape
    owners = lax.axis_size("section")
    tokens_here = token_ids.shape[0]
    cap = 2 * tokens_here // owners
    slot, local = slot_layout(token_ids, owners, cap, rows_own)
    outgoing = jnp.zeros((owners * cap, width), jnp.bfloat16).at[slot].set(embed_grad)
    targets = jnp.full((owners * cap,), -1, jnp.int32).at[slot].set(local)
    got_rows, got_local = (
        lax.all_to_all(
            outgoing.reshape(owners, cap, width), "section", split_axis=0, concat_axis=0, tiled=True
        ),
        lax.all_to_all(
            targets.reshape(owners, cap), "section", split_axis=0, concat_axis=0, tiled=True
        ),
    )
    select = (jnp.arange(rows_own)[:, None] == got_local.reshape(-1)[None, :]).astype(jnp.bfloat16)
    embed_sum = jnp.dot(
        select, got_rows.reshape(owners * cap, width), preferred_element_type=jnp.float32
    )
    grad = proj_grad + embed_sum
    new_param, new_moment_one, new_moment_two = adam(param, moment_one, moment_two, grad)
    table = new_param.astype(jnp.bfloat16)
    piece = lax.all_gather(table, "section", axis=0, tiled=True)
    inside = (next_ids >= 0) & (next_ids < piece.shape[0])
    found = jnp.take(piece, jnp.clip(next_ids, 0, piece.shape[0] - 1), axis=0)
    mine = jnp.where(inside[:, None], found, jnp.zeros((tokens_here, width), jnp.bfloat16))
    next_rows = lax.all_gather(mine, "tp", axis=1, tiled=True)
    return (new_param, new_moment_one, new_moment_two, next_rows)


def solution(mesh):
    placed = (
        P("section", "tp"),
        P("section", "tp"),
        P("section", "tp"),
        P("section", "tp"),
        P("section", "tp"),
        P("section"),
        P("section"),
    )
    ranks = mesh.shape["tp"]

    def on_device(*args):
        owners = mesh.shape["section"]
        table_rows, tokens = args[0].shape[0] * owners, args[5].shape[0]
        if owners == 2 ** 3 and table_rows <= tokens and args[0].shape[0] % 64 == 0 and args[0].shape[1] % 256 in (0, 128):
            return fused(ranks, *args)
        return exchange(*args)

    return jax.shard_map(
        on_device,
        mesh=mesh,
        in_specs=placed,
        out_specs=(P("section", "tp"), P("section", "tp"), P("section", "tp"), P("section", None)),
        check_vma=False,
    )
```

time: 44.4 us -> 36.6 us (0.82); the launches traced: 43.8 us -> 36.5 us
  Pallas kernels: 43.1 us -> 35.8 us
    pallas_call x1, Pallas kernels: 41.1 us -> 33.8 us  [fused(): pl.pallas_call(functools.partial(sync_kernel, ranks), out_shape=(own, own...]
where the time goes in v2:
time: 36.6 us; the launch traced here: 36.5 us
  Pallas kernels  35.8 us (98%)
  between operations  0.64 us (2%)
    pallas_call x1, Pallas kernels, fused(): pl.pallas_call(functools.partial(sync_kernel, ranks), out_shape=(own, own...  33.8 us
    pallas_call x1, Pallas kernels, fused(): pl.pallas_call(hand_over, out_shape=tuple((jax.ShapeDtypeStruct(one.shape...  2.09 us

profile of v2, /device:TPU:0, one launch (start us, length us, event | category | flops | bytes accessed | tf_op | source)
XLA Modules:
  0.0 36.5 jit_solution(13385888816877419223)
XLA Ops:
  0.6 33.8 %shard_map.102 = (f32[64,896]{1,0:T(8,128)S(1)}, f32[64,896]{1,0:T(8,128)S(1)}, f32[64,896]{1,0:T(8,128)S(1)}, bf16[512,3584]{1,0:T(8,128)(2,1)S(1)}) custom-call(s32[1,512]{1,0:T(1,128)} %bitcast.2, s32[1,512]{1,0:T(1,128)} %bitcast.3, bf16[512,896]{1,0:T(8,128)(2,1)} %rows_in.1, f32[64,896]{1,0:T(8,128)} %param_in.1, f32[64,896]{1,0:T(8,128)} %one_in.1, ...), custom_call_target="tpu_custom_call" | custom-call | tf_op jit(solution)/shard_map/pallas_call | solution.py:379
  34.4 2.1 %shard_map.103 = (f32[64,896]{1,0:T(8,128)}, f32[64,896]{1,0:T(8,128)}, f32[64,896]{1,0:T(8,128)}, bf16[512,3584]{1,0:T(8,128)(2,1)}) custom-call(f32[64,896]{1,0:T(8,128)S(1)} %get-tuple-element.8.refs_0_, f32[64,896]{1,0:T(8,128)S(1)} %get-tuple-element.9.refs_1_, f32[64,896]{1,0:T(8,128)S(1)} %get-tuple-element.10.refs_2_, ...), custom_call_target="tpu_custom_call" | custom-call | tf_op jit(solution)/shard_map/pallas_call | solution.py:407
